TPU v7x, 32 devices: a whole 2x2x4 slice. The times are simulated.
32 devices in a mesh: gx: 4 (over y, core), gy: 8 (over z, x).
Axes of the slice: x: 2, y: 2, z: 4, core: 2. Of those that a mesh axis runs over, the one named last changes fastest.
Arguments:
- emission: float32 [512, 8, 128], P(('gx', 'gy')), may hold values from 0.05 to 1
- reflectance: float32 [512, 8, 128], P(('gx', 'gy')), may hold values from 0.5 to 0.98
- form_factors: float32 [8192, 128, 128], P(('gx', 'gy')), as said below
- link_source: int32 [8192], P(('gx', 'gy')), may hold values from 0 to 511, as said below
- link_target: int32 [8192], P(('gx', 'gy')), may hold values from 0 to 511, as said below
- link_length: int32 [8192], P(('gx', 'gy')), may hold values from 32 to 128
- block_count: int32 [32], P(('gx', 'gy')), may hold values from 32 to 256, as said below
Outputs:
- solution: float32 [512, 8, 128], P(('gx', 'gy'))
- residual: float32 [512, 8, 128], P(('gx', 'gy'))
Inputs may be any that keep to these rules, and one draw needn't show every extreme that they name: `form_factors`: entries are nonnegative. `link_source`: block k's source is any cluster; among the blocks held by one device, all blocks whose sources lie on one same device name the same source cluster. `link_target`: block k's target is one of the clusters of the device holding it, clusters (k // 256) * 16 to (k // 256) * 16 + 15. `block_count`: some device has all 256 slots live.
All inputs are finite; a program needn't handle non-finite values.
Results may differ from a plain program's by a relative error of at most 0.0011.
Values sent between devices are 32-bit elements; how exact they have to be, the bound alone decides.
A program may use at most 64 MiB of HBM per device.

v0:
```python
import jax
import jax.numpy as jnp
from jax import lax
from jax.sharding import PartitionSpec as P

ITERS = 3


def local(emission, reflectance, form_factors, link_source, link_target, link_length, block_count):
    clusters = emission.shape[0]
    blocks = form_factors.shape[0]
    patch_count = form_factors.shape[2]
    devices = lax.axis_size(("gx", "gy"))
    group_size = min(16, blocks)
    live_count = block_count[0]
    block_ids = jnp.arange(blocks, dtype=jnp.int32)
    live_block = block_ids < live_count
    owner_dev = link_source // clusters
    local_slot = link_source % clusters
    peer_ids = jnp.arange(devices, dtype=jnp.int32)
    peer_match = (owner_dev[None, :] == peer_ids[:, None]) & live_block[None, :]
    wanted = jnp.max(jnp.where(peer_match, local_slot[None, :], 0), axis=1)
    want_from = lax.all_to_all(wanted, ("gx", "gy"), split_axis=0, concat_axis=0, tiled=True)
    column_ids = jnp.arange(patch_count, dtype=jnp.int32)
    column_mask = ((column_ids[None, :] < link_length[:, None]) & live_block[:, None]).astype(
        jnp.float32
    )
    cluster_ids = jnp.arange(clusters, dtype=jnp.int32)
    target_onehot = (cluster_ids[:, None] == (link_target % clusters)[None, :]).astype(jnp.float32)
    turn_count = (live_count + group_size - 1) // group_size

    def operate(radiance):
        outgoing = radiance[want_from]
        arrived = lax.all_to_all(outgoing, ("gx", "gy"), split_axis=0, concat_axis=0, tiled=True)
        sources = arrived[owner_dev] * column_mask[:, None, :]

        def turn(turn_index, total):
            first_block = turn_index * group_size
            factors = lax.dynamic_slice_in_dim(form_factors, first_block, group_size, 0)
            source_vals = lax.dynamic_slice_in_dim(sources, first_block, group_size, 0)
            onehot_part = lax.dynamic_slice_in_dim(target_onehot, first_block, group_size, 1)
            partial_sum = jnp.einsum(
                "kij,kbj->kbi", factors, source_vals, precision=lax.Precision.HIGHEST
            )
            return total + jnp.dot(
                onehot_part, partial_sum.reshape(group_size, -1), precision=lax.Precision.HIGHEST
            )

        empty_sum = jnp.zeros((clusters, radiance.shape[1] * radiance.shape[2]), jnp.float32)
        gathered = lax.fori_loop(0, turn_count, turn, empty_sum)
        return radiance - reflectance * gathered.reshape(radiance.shape)

    solution = jnp.zeros_like(emission)
    residual = emission
    direction = jnp.zeros_like(emission)
    applied = jnp.zeros_like(emission)
    rho_old = jnp.ones((), jnp.float32)
    alpha_coef = jnp.ones((), jnp.float32)
    omega_coef = jnp.ones((), jnp.float32)
    rho_now = lax.psum(jnp.sum(emission * residual), ("gx", "gy"))
    for iteration in range(ITERS):
        beta_coef = rho_now / rho_old * (alpha_coef / omega_coef)
        direction = residual + beta_coef * (direction - omega_coef * applied)
        applied = operate(direction)
        alpha_coef = rho_now / lax.psum(jnp.sum(emission * applied), ("gx", "gy"))
        middle = residual - alpha_coef * applied
        bounce = operate(middle)
        cross_sum, square_sum, shadow_middle, shadow_bounce = lax.psum(
            (
                jnp.sum(bounce * middle),
                jnp.sum(bounce * bounce),
                jnp.sum(emission * middle),
                jnp.sum(emission * bounce),
            ),
            ("gx", "gy"),
        )
        omega_coef = cross_sum / square_sum
        solution = solution + alpha_coef * direction + omega_coef * middle
        residual = middle - omega_coef * bounce
        rho_old = rho_now
        rho_now = shadow_middle - omega_coef * shadow_bounce
    return (solution, residual)


def solution(mesh):
    in_specs = (
        P(("gx", "gy"), None, None),
        P(("gx", "gy"), None, None),
        P(("gx", "gy"), None, None),
        P(("gx", "gy")),
        P(("gx", "gy")),
        P(("gx", "gy")),
        P(("gx", "gy")),
    )
    out_specs = (P(("gx", "gy"), None, None), P(("gx", "gy"), None, None))
    return jax.shard_map(local, mesh=mesh, in_specs=in_specs, out_specs=out_specs, check_vma=False)
```

profile of v0, /device:TPU:0, one launch (start us, length us, event | category | flops | bytes accessed | tf_op | source)
XLA Modules:
  0.0 709.3 jit_solution(13711820568220223381)
XLA Ops:
  4.4 7.3 %all-to-all-start = ((s32[32,1,1]{2,1,0:T(1,128)}), s32[32,1,1]{2,1,0:T(1,128)S(1)}, u32[]{:S(2)}, u32[]{:S(2)}) async-start(s32[32,1,1]{2,1,0:T(1,128)} %copy.11), calls=%async_computation | async-start | bytes 32768 | tf_op jit(solution)/shard_map/all_to_all | solution.py:23
  11.7 40.7 %psum.98 = f32[]{:T(128)} all-reduce(f32[]{:T(128)} %multiply_reduce_fusion.13), channel_id=1, replica_groups=mesh['gx'=4,'gy'=8] {'gx','gy'}, use_global_device_ids=true, to_apply=%region_1.2 | all-reduce | flops 1 | bytes 8 | tf_op jit(solution)/shard_map/psum | solution.py:60
  56.6 4.7 all-to-all-start.1
  62.2 7.0 all-to-all-done.1
  70.3 35.9 %while.60 = (s32[]{:T(128)}, f32[16,1024]{1,0:T(8,128)S(1)}, s32[]{:T(128)}, f32[16,256]{1,0:T(8,128)S(1)}, f32[256,8,128]{2,1,0:T(8,128)S(1)}, /*index=5*/f32[2...) while((s32[]{:T(128)}, f32[16,1024]{1,0:T(8,128)S(1)}, s32[]{:T(128)}, ...), condition=%wide.region_4.5_spmd, body=%wide.region_3.4_spmd.sunk | while | flops 28327940 | bytes 1385623 | solution.py:50
  107.7 55.0 %psum.99 = f32[]{:T(128)} all-reduce(f32[]{:T(128)} %get-tuple-element.303), channel_id=1, replica_groups=mesh['gx'=4,'gy'=8] {'gx','gy'}, use_global_device_ids=true, to_apply=%region_6.7 | all-reduce | flops 1 | bytes 8 | tf_op jit(solution)/shard_map/psum | solution.py:65
  166.2 4.1 all-to-all-start.2
  170.4 7.8 %all-to-all-done.2 = f32[32,8,128]{2,1,0:T(8,128)S(1)} async-done(((f32[32,8,128]{2,1,0:T(8,128)}), f32[32,8,128]{2,1,0:T(8,128)S(1)}, u32[]{:S(2)}, u32[]{:S(2)}) %all-to-all-start.2) | async-done | bytes 131104 | tf_op jit(solution)/shard_map/all_to_all | solution.py:34
  179.3 35.9 %while.61 = (s32[]{:T(128)}, f32[16,1024]{1,0:T(8,128)S(1)}, s32[]{:T(128)}, f32[16,256]{1,0:T(8,128)S(1)}, f32[256,8,128]{2,1,0:T(8,128)S(1)}, /*index=5*/f32[2...) while((s32[]{:T(128)}, f32[16,1024]{1,0:T(8,128)S(1)}, s32[]{:T(128)}, ...), condition=%wide.region_8.9_spmd, body=%wide.region_7.8_spmd.sunk | while | flops 28327940 | bytes 1385623 | solution.py:50
  216.0 55.2 %all-reduce.2 = (f32[]{:T(128)}, f32[]{:T(128)}, f32[]{:T(128)}, f32[]{:T(128)}) all-reduce(f32[]{:T(128)} %get-tuple-element.215, f32[]{:T(128)} %get-tuple-element.214, f32[]{:T(128)} %get-tuple-element.213, f32[]{:T(128)} %get-tuple-element.212), channel_id=1, replica_groups=mesh['gx'=4,'gy'=8] {'gx','gy'}, use_global_device_ids=true, to_apply=%region_14.15 | all-reduce | flops 4 | bytes 32 | tf_op jit(solution)/shard_map/psum | solution.py:68
  278.2 4.2 all-to-all-start.3
  282.4 7.8 %all-to-all-done.3 = f32[32,8,128]{2,1,0:T(8,128)S(1)} async-done(((f32[32,8,128]{2,1,0:T(8,128)}), f32[32,8,128]{2,1,0:T(8,128)S(1)}, u32[]{:S(2)}, u32[]{:S(2)}) %all-to-all-start.3) | async-done | bytes 131104 | tf_op jit(solution)/shard_map/all_to_all | solution.py:34
  291.4 35.9 %while.62 = (s32[]{:T(128)}, f32[16,1024]{1,0:T(8,128)S(1)}, s32[]{:T(128)}, f32[16,256]{1,0:T(8,128)S(1)}, f32[256,8,128]{2,1,0:T(8,128)S(1)}, /*index=5*/f32[2...) while((s32[]{:T(128)}, f32[16,1024]{1,0:T(8,128)S(1)}, s32[]{:T(128)}, ...), condition=%wide.region_18.19_spmd, body=%wide.region_17.18_spmd.sunk | while | flops 28327940 | bytes 1385623 | solution.py:50
  328.0 55.0 %psum.104 = f32[]{:T(128)} all-reduce(f32[]{:T(128)} %get-tuple-element.300), channel_id=1, replica_groups=mesh['gx'=4,'gy'=8] {'gx','gy'}, use_global_device_ids=true, to_apply=%region_20.21 | all-reduce | flops 1 | bytes 8 | tf_op jit(solution)/shard_map/psum | solution.py:65
  389.1 7.8 %all-to-all-done.4 = f32[32,8,128]{2,1,0:T(8,128)S(1)} async-done(((f32[32,8,128]{2,1,0:T(8,128)}), f32[32,8,128]{2,1,0:T(8,128)S(1)}, u32[]{:S(2)}, u32[]{:S(2)}) %all-to-all-start.4) | async-done | bytes 131104 | tf_op jit(solution)/shard_map/all_to_all | solution.py:34
  398.1 36.1 %while.63 = (s32[]{:T(128)}, f32[16,1024]{1,0:T(8,128)S(1)}, s32[]{:T(128)}, f32[16,256]{1,0:T(8,128)S(1)}, f32[256,8,128]{2,1,0:T(8,128)S(1)}, /*index=5*/f32[2...) while((s32[]{:T(128)}, f32[16,1024]{1,0:T(8,128)S(1)}, s32[]{:T(128)}, ...), condition=%wide.region_22.23_spmd, body=%wide.region_21.22_spmd.sunk | while | flops 28327940 | bytes 1385623 | solution.py:50
  434.9 55.2 %all-reduce.1 = (f32[]{:T(128)}, f32[]{:T(128)}, f32[]{:T(128)}, f32[]{:T(128)}) all-reduce(f32[]{:T(128)} %get-tuple-element.211, f32[]{:T(128)} %get-tuple-element.210, f32[]{:T(128)} %get-tuple-element.209, f32[]{:T(128)} %get-tuple-element.208), channel_id=1, replica_groups=mesh['gx'=4,'gy'=8] {'gx','gy'}, use_global_device_ids=true, to_apply=%region_28.29 | all-reduce | flops 4 | bytes 32 | tf_op jit(solution)/shard_map/psum | solution.py:68
  495.8 4.2 all-to-all-start.5
  500.0 7.8 %all-to-all-done.5 = f32[32,8,128]{2,1,0:T(8,128)S(1)} async-done(((f32[32,8,128]{2,1,0:T(8,128)}), f32[32,8,128]{2,1,0:T(8,128)S(1)}, u32[]{:S(2)}, u32[]{:S(2)}) %all-to-all-start.5) | async-done | bytes 131104 | tf_op jit(solution)/shard_map/all_to_all | solution.py:34
  508.9 35.9 %while.64 = (s32[]{:T(128)}, f32[16,1024]{1,0:T(8,128)S(1)}, s32[]{:T(128)}, f32[16,256]{1,0:T(8,128)S(1)}, f32[256,8,128]{2,1,0:T(8,128)S(1)}, /*index=5*/f32[2...) while((s32[]{:T(128)}, f32[16,1024]{1,0:T(8,128)S(1)}, s32[]{:T(128)}, ...), condition=%wide.region_32.33_spmd, body=%wide.region_31.32_spmd.sunk | while | flops 28327940 | bytes 1385623 | solution.py:50
  545.5 55.0 %psum.109 = f32[]{:T(128)} all-reduce(f32[]{:T(128)} %multiply_reduce_fusion.2), channel_id=1, replica_groups=mesh['gx'=4,'gy'=8] {'gx','gy'}, use_global_device_ids=true, to_apply=%region_34.35 | all-reduce | flops 1 | bytes 8 | tf_op jit(solution)/shard_map/psum | solution.py:65
  606.6 7.8 %all-to-all-done.6 = f32[32,8,128]{2,1,0:T(8,128)S(1)} async-done(((f32[32,8,128]{2,1,0:T(8,128)}), f32[32,8,128]{2,1,0:T(8,128)S(1)}, u32[]{:S(2)}, u32[]{:S(2)}) %all-to-all-start.6) | async-done | bytes 131104 | tf_op jit(solution)/shard_map/all_to_all | solution.py:34
  615.6 35.9 %while.65 = (s32[]{:T(128)}, f32[16,1024]{1,0:T(8,128)S(1)}, s32[]{:T(128)}, f32[16,256]{1,0:T(8,128)S(1)}, f32[256,8,128]{2,1,0:T(8,128)S(1)}, /*index=5*/f32[2...) while((s32[]{:T(128)}, f32[16,1024]{1,0:T(8,128)S(1)}, s32[]{:T(128)}, ...), condition=%wide.region_36.37_spmd, body=%wide.region_35.36_spmd.sunk | while | flops 28327940 | bytes 1385623 | solution.py:50
  652.2 55.1 %all-reduce = (f32[]{:T(128)}, f32[]{:T(128)}) all-reduce(f32[]{:T(128)} %get-tuple-element.207, f32[]{:T(128)} %get-tuple-element.206), channel_id=1, replica_groups=mesh['gx'=4,'gy'=8] {'gx','gy'}, use_global_device_ids=true, to_apply=%region_38.39 | all-reduce | flops 2 | bytes 16 | tf_op jit(solution)/shard_map/psum | solution.py:68
  (194 shorter events, 248.5 us)
Async XLA Ops:
  0.6 214.7 %copy-start = (f32[16,8,128]{2,1,0:T(8,128)S(1)}, f32[16,8,128]{2,1,0:T(8,128)}, u32[]{:S(2)}) copy-start(f32[16,8,128]{2,1,0:T(8,128)} %param.19) | copy-start | bytes 196612
  0.6 214.7 %copy-start.1 = (f32[16,8,128]{2,1,0:T(8,128)S(1)}, f32[16,8,128]{2,1,0:T(8,128)}, u32[]{:S(2)}) copy-start(f32[16,8,128]{2,1,0:T(8,128)} %param.20) | copy-start | bytes 196612
  4.4 50.3 %all-to-all-start = ((s32[32,1,1]{2,1,0:T(1,128)}), s32[32,1,1]{2,1,0:T(1,128)S(1)}, u32[]{:S(2)}, u32[]{:S(2)}) async-start(s32[32,1,1]{2,1,0:T(1,128)} %copy.11), calls=%async_computation | async-start | bytes 32768 | tf_op jit(solution)/shard_map/all_to_all | solution.py:23
  56.6 12.6 %all-to-all-start.1 = ((f32[32,8,128]{2,1,0:T(8,128)}), f32[32,8,128]{2,1,0:T(8,128)S(1)}, u32[]{:S(2)}, u32[]{:S(2)}) async-start(f32[32,8,128]{2,1,0:T(8,128)} %gather_fusion), calls=%async_computation.1 | async-start | bytes 262144 | tf_op jit(solution)/shard_map/all_to_all | solution.py:34
  166.2 12.0 %all-to-all-start.2 = ((f32[32,8,128]{2,1,0:T(8,128)}), f32[32,8,128]{2,1,0:T(8,128)S(1)}, u32[]{:S(2)}, u32[]{:S(2)}) async-start(f32[32,8,128]{2,1,0:T(8,128)} %gather_fusion.2), calls=%async_computation.2 | async-start | bytes 262144 | tf_op jit(solution)/shard_map/all_to_all | solution.py:34
  278.2 12.0 %all-to-all-start.3 = ((f32[32,8,128]{2,1,0:T(8,128)}), f32[32,8,128]{2,1,0:T(8,128)S(1)}, u32[]{:S(2)}, u32[]{:S(2)}) async-start(f32[32,8,128]{2,1,0:T(8,128)} %gather_fusion.4), calls=%async_computation.3 | async-start | bytes 262144 | tf_op jit(solution)/shard_map/all_to_all | solution.py:34
  384.9 12.0 %all-to-all-start.4 = ((f32[32,8,128]{2,1,0:T(8,128)}), f32[32,8,128]{2,1,0:T(8,128)S(1)}, u32[]{:S(2)}, u32[]{:S(2)}) async-start(f32[32,8,128]{2,1,0:T(8,128)} %gather_fusion.6), calls=%async_computation.4 | async-start | bytes 262144 | tf_op jit(solution)/shard_map/all_to_all | solution.py:34
  495.8 12.0 %all-to-all-start.5 = ((f32[32,8,128]{2,1,0:T(8,128)}), f32[32,8,128]{2,1,0:T(8,128)S(1)}, u32[]{:S(2)}, u32[]{:S(2)}) async-start(f32[32,8,128]{2,1,0:T(8,128)} %gather_fusion.8), calls=%async_computation.5 | async-start | bytes 262144 | tf_op jit(solution)/shard_map/all_to_all | solution.py:34
  602.5 12.0 %all-to-all-start.6 = ((f32[32,8,128]{2,1,0:T(8,128)}), f32[32,8,128]{2,1,0:T(8,128)S(1)}, u32[]{:S(2)}, u32[]{:S(2)}) async-start(f32[32,8,128]{2,1,0:T(8,128)} %gather_fusion.10), calls=%async_computation.6 | async-start | bytes 262144 | tf_op jit(solution)/shard_map/all_to_all | solution.py:34
where the time goes:
time: 714 us; the launch traced here: 709 us
  blocking collectives  371 us (52%)
  matrix products  213 us (30%)
  waiting for transfers between devices  46 us (6%)
  starting transfers between devices  32.9 us (5%)
  between operations  16.7 us (2%)
  local copies, waits for them, and re-layouts  14.3 us (2%)
  other arithmetic  12.4 us (2%)
    dot_general x66, matrix products, turn(): jnp.einsum('kij,kbj->kbi', factors, source_vals, precision=lax.Precision....  195 us
    psum x3, blocking collectives, local(): lax.psum((jnp.sum(bounce * middle), jnp.sum(bounce * bounce), jnp.sum(emi...  165 us
    psum x3, blocking collectives, local(): alpha_coef = rho_now / lax.psum(jnp.sum(emission * applied), ('gx', 'gy'))  165 us
    all_to_all x6, waiting for transfers between devices, operate(): lax.all_to_all(outgoing, ('gx', 'gy'), split_axis=0, concat_axis=0, tiled...  46 us
    psum x1, blocking collectives, local(): rho_now = lax.psum(jnp.sum(emission * residual), ('gx', 'gy'))  40.7 us
    all_to_all x6, starting transfers between devices, operate(): lax.all_to_all(outgoing, ('gx', 'gy'), split_axis=0, concat_axis=0, tiled...  25.6 us
    dot_general x66, matrix products, turn(): jnp.dot(onehot_part, partial_sum.reshape(group_size, -1), precision=lax.P...  18.5 us
  transfers between devices with their start and end apart: 7, of which 6 were waited for; matrix products, arithmetic and copies ran while one was open for 0% of the time, Pallas kernels for 0%

commit v1 on v0

v1 whole, which is shorter than its diff:
```python
import jax
import jax.numpy as jnp
from jax import lax
from jax.sharding import PartitionSpec as P
from jax.experimental import pallas as pl
from jax.experimental.pallas import tpu as pltpu

ITERS = 3
PHASES = 2 * ITERS + 1
CHUNK = 16
SLOTS = 4
UNROLL = 16


def kernel(perm_s, own_s, len_s, keep_s, end_s, val_s, want_s, em, refl, ff, sol, res,
           w, stage, runs, vt, outb, inb, dout, din, image, direction, total, rs, ds, ims,
           stage_sem, send_sem, recv_sem, dsend_sem, drecv_sem):
    nx, ny = lax.axis_size("gx"), lax.axis_size("gy")
    n = nx * ny
    me = lax.axis_index("gx") * ny + lax.axis_index("gy")
    clusters = em.shape[0]
    blocks, cl = ff.shape[0], ff.shape[2]
    chunks = blocks // CHUNK
    f32, bf16 = jnp.float32, jnp.bfloat16

    def fetch(c, slot):
        return pltpu.make_async_copy(ff.at[pl.ds(c * CHUNK, CHUNK)], stage.at[slot], stage_sem.at[slot])

    for c in range(min(SLOTS, chunks)):
        fetch(c, c).start()

    barrier = pltpu.get_barrier_semaphore()

    def greet(r, carry):
        peer = lax.rem(me + r, n)
        pl.semaphore_signal(barrier, inc=1, device_id=(peer // ny, lax.rem(peer, ny)),
                            device_id_type=pl.DeviceIdType.MESH)
        return carry

    lax.fori_loop(1, n, greet, 0)
    pl.semaphore_wait(barrier, n - 1)

    lane = lax.broadcasted_iota(jnp.int32, (1, 128), 1)

    def dot(a, b):
        part = jnp.sum(a * b, axis=0)
        part = jnp.sum(part, axis=0, keepdims=True)
        return jnp.sum(part, axis=1, keepdims=True)

    def send(phase, field, pairs):
        if field is not None:
            def one(r, carry):
                peer = lax.rem(me + r, n)
                outb[phase, peer] = field[want_s[peer]]
                pltpu.make_async_remote_copy(
                    src_ref=outb.at[phase, peer], dst_ref=inb.at[phase, me],
                    send_sem=send_sem.at[phase], recv_sem=recv_sem.at[phase],
                    device_id=(peer // ny, lax.rem(peer, ny)),
                    device_id_type=pl.DeviceIdType.MESH).start()
                return carry

            lax.fori_loop(1, n, one, 0)
            inb[phase, me] = field[want_s[me]]
        row = jnp.zeros((1, 128), f32)
        for i, (a, b) in enumerate(pairs):
            row = jnp.where(lane == i, jnp.broadcast_to(dot(a[...], b[...]), (1, 128)), row)
        dout[phase] = row
        din[phase, me] = row

        def two(r, carry):
            peer = lax.rem(me + r, n)
            pltpu.make_async_remote_copy(
                src_ref=dout.at[phase], dst_ref=din.at[phase, me],
                send_sem=dsend_sem.at[phase], recv_sem=drecv_sem.at[phase],
                device_id=(peer // ny, lax.rem(peer, ny)),
                device_id_type=pl.DeviceIdType.MESH).start()
            return carry

        lax.fori_loop(1, n, two, 0)

    def drain(ref, sem):
        part = ref.at[pl.ds(0, n - 1)]
        pltpu.make_async_copy(part, part, sem).wait()

    def receive(phase, count, rows):
        drain(din.at[phase], drecv_sem.at[phase])
        drain(din.at[phase], dsend_sem.at[phase])
        sums = jnp.sum(din[phase], axis=0)
        if rows:
            drain(inb.at[phase], recv_sem.at[phase])
            drain(outb.at[phase], send_sem.at[phase])
        return [jnp.broadcast_to(jnp.sum(jnp.where(lane == i, sums, 0.0), axis=1, keepdims=True), (8, 128))
                for i in range(count)]

    def put_sources(v):
        low = v - v.astype(bf16).astype(f32)
        vt[...] = jnp.concatenate([v, low], axis=1).astype(bf16)

    def apply(v):
        def step(s, acc):
            for u in range(UNROLL // 2):
                r = s * UNROLL + 2 * u
                va, vb = vt[own_s[r]], vt[own_s[r + 1]]
                left = jnp.concatenate([jnp.concatenate([va, va], axis=1),
                                        jnp.concatenate([vb, vb], axis=1)], axis=0)
                right = jnp.concatenate([w[perm_s[r]], w[perm_s[r + 1]]], axis=1)
                out = jnp.dot(left, right, preferred_element_type=f32)
                acc = acc * keep_s[r] + (out[0:8, :cl] + out[8:16, :cl])
                runs[r] = acc
                acc = acc * keep_s[r + 1] + (out[16:24, cl:] + out[24:32, cl:])
                runs[r + 1] = acc
            return acc

        lax.fori_loop(0, blocks // UNROLL, step, jnp.zeros((8, cl), f32))
        g = jnp.stack([runs[end_s[t]] * val_s[t] for t in range(clusters)])
        return v - refl[...] * g

    send(0, em, [(em, em)])

    def prepare(c, carry):
        slot = lax.rem(c, SLOTS)
        fetch(c, slot).wait()

        def block(b, inner):
            k = c * CHUNK + b
            t = stage[slot, b].T
            j = lax.broadcasted_iota(jnp.int32, (cl, cl), 0)
            t = jnp.where(j < len_s[k], t, 0.0)
            high = t.astype(bf16)
            w[k, 0:cl] = high
            w[k, cl:2 * cl] = (t - high.astype(f32)).astype(bf16)
            return inner

        lax.fori_loop(0, CHUNK, block, 0, unroll=4)

        @pl.when(c + SLOTS < chunks)
        def _():
            fetch(c + SLOTS, slot).start()

        return carry

    lax.fori_loop(0, chunks, prepare, 0)

    (rho,) = receive(0, 1, True)
    rs[...] = inb[0]
    res[...] = em[...]
    rho_old, alpha, omega = None, None, None
    for it in range(ITERS):
        last = it == ITERS - 1
        if it == 0:
            direction[...] = em[...]
            ds[...] = rs[...]
        else:
            beta = rho / rho_old * (alpha / omega)
            direction[...] = res[...] + beta * (direction[...] - omega * image[...])
            ds[...] = rs[...] + beta * (ds[...] - omega * ims[...])
        put_sources(ds[...])
        image[...] = apply(direction[...])
        phase = 1 + 2 * it
        send(phase, image, [(em, image)])
        (sim,) = receive(phase, 1, True)
        alpha = rho / sim
        ims[...] = inb[phase]
        res[...] = res[...] - alpha * image[...]
        rs[...] = rs[...] - alpha * ims[...]
        put_sources(rs[...])
        sol[...] = apply(res[...])
        send(phase + 1, None if last else sol, [(sol, res), (sol, sol), (em, res), (em, sol)])
        cross, square, sm, sb = receive(phase + 1, 4, not last)
        omega = cross / square
        if it == 0:
            total[...] = alpha * direction[...] + omega * res[...]
        else:
            total[...] = total[...] + alpha * direction[...] + omega * res[...]
        res[...] = res[...] - omega * sol[...]
        if not last:
            rs[...] = rs[...] - omega * inb[phase + 1]
        rho_old = rho
        rho = sm - omega * sb
    sol[...] = total[...]


def local(emission, reflectance, form_factors, link_source, link_target, link_length, block_count):
    clusters, bands, cl = emission.shape
    blocks = form_factors.shape[0]
    devices = lax.axis_size(("gx", "gy"))
    i32, f32, bf16 = jnp.int32, jnp.float32, jnp.bfloat16
    ids = jnp.arange(blocks, dtype=i32)
    live = ids < block_count[0]
    owner = link_source // clusters
    slot = link_source % clusters
    peers = jnp.arange(devices, dtype=i32)
    match = (owner[None, :] == peers[:, None]) & live[None, :]
    wanted = jnp.max(jnp.where(match, slot[None, :], 0), axis=1)
    want = lax.all_to_all(wanted, ("gx", "gy"), split_axis=0, concat_axis=0, tiled=True)
    length = jnp.where(live, link_length, 0)
    target = link_target % clusters
    key = target * blocks + ids
    rank = jnp.sum((key[None, :] < key[:, None]).astype(i32), axis=1)
    place = rank[None, :] == ids[:, None]
    perm = jnp.sum(jnp.where(place, ids[None, :], 0), axis=1)
    own = jnp.sum(jnp.where(place, owner[None, :], 0), axis=1)
    sorted_target = jnp.sum(jnp.where(place, target[None, :], 0), axis=1)
    before = jnp.concatenate([jnp.full((1,), -1, i32), sorted_target[:-1]])
    keep = (before == sorted_target).astype(f32)
    cids = jnp.arange(clusters, dtype=i32)
    end = jnp.maximum(jnp.sum((target[None, :] <= cids[:, None]).astype(i32), axis=1) - 1, 0)
    valid = jnp.any(target[None, :] == cids[:, None], axis=1).astype(f32)
    smem = pl.BlockSpec(memory_space=pltpu.SMEM)
    vmem = pl.BlockSpec(memory_space=pltpu.VMEM)
    field = (clusters, bands, cl)
    rows = (devices, bands, cl)
    dma = pltpu.SemaphoreType.DMA
    return pl.pallas_call(
        kernel,
        out_shape=[jax.ShapeDtypeStruct(field, f32)] * 2,
        in_specs=[smem] * 7 + [vmem, vmem, pl.BlockSpec(memory_space=pl.ANY)],
        out_specs=[vmem, vmem],
        scratch_shapes=[
            pltpu.VMEM((blocks, 2 * cl, cl), bf16),
            pltpu.VMEM((SLOTS, CHUNK, cl, cl), f32),
            pltpu.VMEM((blocks, bands, cl), f32),
            pltpu.VMEM((devices, 2 * bands, cl), bf16),
            pltpu.VMEM((PHASES - 1,) + rows, f32),
            pltpu.VMEM((PHASES - 1,) + rows, f32),
            pltpu.VMEM((PHASES, 1, 128), f32),
            pltpu.VMEM((PHASES, devices, 1, 128), f32),
            pltpu.VMEM(field, f32),
            pltpu.VMEM(field, f32),
            pltpu.VMEM(field, f32),
            pltpu.VMEM(rows, f32),
            pltpu.VMEM(rows, f32),
            pltpu.VMEM(rows, f32),
            dma((SLOTS,)),
            dma((PHASES,)),
            dma((PHASES,)),
            dma((PHASES,)),
            dma((PHASES,)),
        ],
        compiler_params=pltpu.CompilerParams(
            collective_id=0, has_side_effects=True, vmem_limit_bytes=56 * 1024 * 1024),
        name="radiosity",
    )(perm, own, length, keep, end, valid, want, emission, reflectance, form_factors)


def solution(mesh):
    wide = P(("gx", "gy"), None, None)
    flat = P(("gx", "gy"))
    return jax.shard_map(local, mesh=mesh, in_specs=(wide, wide, wide, flat, flat, flat, flat),
                         out_specs=(wide, wide), check_vma=False)
```

time: 714 us -> 101 us (0.14)
  blocking collectives: 371 us -> 0 us
  matrix products: 213 us -> 0 us
  Pallas kernels: 0 us -> 78.9 us
  waiting for transfers between devices: 46 us -> 2.84 us
  starting transfers between devices: 32.9 us -> 7.33 us
  between operations: 16.7 us -> 1.31 us
  local copies, waits for them, and re-layouts: 14.3 us -> 3.64 us
    psum x7 -> x0, blocking collectives: 371 us -> none  [the longest x3 165 us: local(): lax.psum((jnp.sum(bounce * middle), jnp.sum(bounce * bounce), jnp.sum(emi...]
    dot_general x132 -> x0, matrix products: 213 us -> none  [the longest x66 195 us: turn(): jnp.einsum('kij,kbj->kbi', factors, source_vals, precision=lax.Precision....]
    pallas_call x0 -> x1, Pallas kernels: none -> 78.9 us  [local(): pl.pallas_call(kernel, out_shape=[jax.ShapeDtypeStruct(field, f32)] * 2,...]
    all_to_all x6 -> x0, waiting for transfers between devices: 46 us -> none  [operate(): lax.all_to_all(outgoing, ('gx', 'gy'), split_axis=0, concat_axis=0, tiled...]
    all_to_all x6 -> x0, starting transfers between devices: 25.6 us -> none  [operate(): lax.all_to_all(outgoing, ('gx', 'gy'), split_axis=0, concat_axis=0, tiled...]
    gather x12 -> x0, local copies, waits for them, and re-layouts: 13.5 us -> none  [the longest x6 7.33 us: operate(): outgoing = radiance[want_from]]
  transfers between devices with their start and end apart: 7 -> 1, of which waited for: 6 -> 1; matrix products, arithmetic and copies ran while one was open for 0% -> 4% of each run, Pallas kernels for 0% -> 0%
where the time goes in v1:
time: 101 us; the launch traced here: 100 us
  Pallas kernels  78.9 us (78%)
  starting transfers between devices  7.33 us (7%)
  other arithmetic  6.24 us (6%)
  local copies, waits for them, and re-layouts  3.64 us (4%)
  waiting for transfers between devices  2.84 us (3%)
  between operations  1.31 us (1%)
    pallas_call x1, Pallas kernels, local(): pl.pallas_call(kernel, out_shape=[jax.ShapeDtypeStruct(field, f32)] * 2,...  78.9 us
    all_to_all x1, starting transfers between devices, local(): lax.all_to_all(wanted, ('gx', 'gy'), split_axis=0, concat_axis=0, tiled=T...  7.33 us
    unnamed x2, local copies, waits for them, and re-layouts  2.95 us
    all_to_all x1, waiting for transfers between devices, local(): lax.all_to_all(wanted, ('gx', 'gy'), split_axis=0, concat_axis=0, tiled=T...  2.84 us
  transfers between devices with their start and end apart: 1, of which 1 were waited for; matrix products, arithmetic and copies ran while one was open for 4% of the time, Pallas kernels for 0%

profile of v1, /device:TPU:0, one launch (start us, length us, event | category | flops | bytes accessed | tf_op | source)
XLA Modules:
  0.0 100.3 jit_solution(9168073629612936731)
XLA Ops:
  1.3 0.7 and_select_fusion
  2.0 0.1 select_reduce_fusion.3
  2.1 0.7 copy.11
  2.8 7.3 %all-to-all-start = ((s32[32,1,1]{2,1,0:T(1,128)}), s32[32,1,1]{2,1,0:T(1,128)S(1)}, u32[]{:S(2)}, u32[]{:S(2)}) async-start(s32[32,1,1]{2,1,0:T(1,128)} %copy.11), calls=%async_computation | async-start | bytes 32768 | tf_op jit(solution)/shard_map/all_to_all | solution.py:195
  10.2 0.1 convert_reduce_fusion.1
  10.3 0.5 add_maximum_fusion.end_s
  10.8 0.2 convert_reduce_fusion
  11.0 0.8 select_reduce_fusion
  11.8 1.3 %broadcast_select_fusion.len_s = s32[256]{0:T(256)} fusion(s32[256]{0:T(256)} %param.12, s32[]{:T(128)} %bitcast.4), kind=kLoop, calls=%fused_computation.27 | loop fusion | flops 512 | bytes 2052 | tf_op jit(solution)/shard_map/jit(_where)/select_n | solution.py:196
  13.1 0.6 compare_convert_fusion.keep_s
  13.7 0.1 fusion.1
  13.8 0.6 convert_element_type.15.val_s
  14.4 2.8 %all-to-all-done = s32[32,1,1]{2,1,0:T(1,128)S(1)} async-done(((s32[32,1,1]{2,1,0:T(1,128)}), s32[32,1,1]{2,1,0:T(1,128)S(1)}, u32[]{:S(2)}, u32[]{:S(2)}) %all-to-all-start) | async-done | bytes 160 | tf_op jit(solution)/shard_map/all_to_all | solution.py:195
  17.2 1.2 %reduce.want_s = s32[32]{0:T(128)} reduce(s32[32,1,1]{2,1,0:T(1,128)S(1)} %all-to-all-done, s32[]{:T(128)} %constant.35.clone.1), dimensions={1,2}, to_apply=%all_to_all.8.reduce_sub_computation | reduce | bytes 260 | tf_op jit(solution)/shard_map/all_to_all | solution.py:195
  18.4 78.9 %radiosity.1 = (f32[16,8,128]{2,1,0:T(8,128)}, f32[16,8,128]{2,1,0:T(8,128)}) custom-call(s32[256]{0:T(256)} %get-tuple-element.4.perm_s, s32[256]{0:T(256)} %get-tuple-element.3.own_s, s32[256]{0:T(256)} %broadcast_select_fusion.len_s, f32[256]{0:T(256)} %compare_convert_fusion.keep_s, s32[16]{0:T(128)} %add_maximum_fusion.end_s, ...), custom_call_target="tpu_custom_call" | custom-call | tf_op jit(solution)/shard_map/radiosity/pallas_call | solution.py:214
  97.3 1.5 %copy.15 = f32[16,8,128]{2,1,0:T(8,128)} copy(f32[16,8,128]{2,1,0:T(8,128)} %get-tuple-element.13) | data formatting | bytes 131072
  98.8 1.5 %copy.16 = f32[16,8,128]{2,1,0:T(8,128)} copy(f32[16,8,128]{2,1,0:T(8,128)} %get-tuple-element.14) | data formatting | bytes 131072
  (1 shorter events, 0.0 us)
Async XLA Ops:
  2.8 14.4 %all-to-all-start = ((s32[32,1,1]{2,1,0:T(1,128)}), s32[32,1,1]{2,1,0:T(1,128)S(1)}, u32[]{:S(2)}, u32[]{:S(2)}) async-start(s32[32,1,1]{2,1,0:T(1,128)} %copy.11), calls=%async_computation | async-start | bytes 32768 | tf_op jit(solution)/shard_map/all_to_all | solution.py:195

commit v2 on v1

--- a/solution.py
+++ b/solution.py
@@ -9,12 +9,20 @@
 PHASES = 2 * ITERS + 1
 CHUNK = 16
 SLOTS = 4
-UNROLL = 16
-
-
-def kernel(perm_s, own_s, len_s, keep_s, end_s, val_s, want_s, em, refl, ff, sol, res,
+UNROLL = 64
+EARLY = 4
+
+
+def divide(x, by):
+    if by & (by - 1) == 0:
+        return lax.shift_right_logical(x, by.bit_length() - 1), lax.bitwise_and(x, by - 1)
+    return lax.div(x, by), lax.rem(x, by)
+
+
+def kernel(len_s, count_s, source_v, target_v, count_v, em, refl, ff, sol, res,
            w, stage, runs, vt, outb, inb, dout, din, image, direction, total, rs, ds, ims,
-           stage_sem, send_sem, recv_sem, dsend_sem, drecv_sem):
+           wout, win, want_s, ints_v, ints_s, reals_v, reals_s,
+           stage_sem, send_sem, recv_sem, dsend_sem, drecv_sem, wsend_sem, wrecv_sem, small_sem):
     nx, ny = lax.axis_size("gx"), lax.axis_size("gy")
     n = nx * ny
     me = lax.axis_index("gx") * ny + lax.axis_index("gy")
@@ -38,7 +46,60 @@
         return carry
 
     lax.fori_loop(1, n, greet, 0)
+
+    i32 = jnp.int32
+    owner, slot = divide(source_v[...], clusters)
+    target = target_v[...] - me * clusters
+    ids = lax.broadcasted_iota(i32, (1, blocks), 1)
+    peers = lax.broadcasted_iota(i32, (n, blocks), 0)
+    alive = jnp.broadcast_to(ids < count_v[:, 0:1], (n, blocks))
+    match = jnp.logical_and(owner == peers, alive)
+    wanted = jnp.max(jnp.where(match, jnp.broadcast_to(slot, (n, blocks)), 0), axis=1, keepdims=True)
+    wout[...] = jnp.broadcast_to(wanted, (n, 128)).reshape(n, 1, 128)
     pl.semaphore_wait(barrier, n - 1)
+
+    def ask(r, carry):
+        peer = lax.rem(me + r, n)
+        pltpu.make_async_remote_copy(
+            src_ref=wout.at[peer], dst_ref=win.at[me], send_sem=wsend_sem, recv_sem=wrecv_sem,
+            device_id=(peer // ny, lax.rem(peer, ny)),
+            device_id_type=pl.DeviceIdType.MESH).start()
+        return carry
+
+    lax.fori_loop(1, n, ask, 0)
+    win[me] = wout[me]
+
+    square_of = (blocks, blocks)
+    down = lax.broadcasted_iota(i32, square_of, 0)
+    across = lax.broadcasted_iota(i32, square_of, 1)
+
+    def upright(row):
+        return jnp.sum(jnp.where(down == across, jnp.broadcast_to(row, square_of), 0), axis=1, keepdims=True)
+
+    key = target * blocks + ids
+    key_up, owner_up, target_up = upright(key), upright(owner), upright(target)
+    rank = jnp.sum((jnp.broadcast_to(key, square_of) < key_up).astype(i32), axis=1, keepdims=True)
+    placed = rank == across
+
+    def ordered(column):
+        return jnp.sum(jnp.where(placed, column, 0), axis=0, keepdims=True)
+
+    sorted_target = ordered(jnp.broadcast_to(target_up, square_of))
+    ints_v[...] = jnp.zeros(ints_v.shape, i32)
+    reals_v[...] = jnp.zeros(reals_v.shape, f32)
+    ints_v[0:1, :] = ordered(down)
+    ints_v[1:2, :] = ordered(jnp.broadcast_to(owner_up, square_of))
+    up_to = jnp.sum((target_up <= across).astype(i32), axis=0, keepdims=True)
+    same = jnp.sum((target_up == across).astype(i32), axis=0, keepdims=True)
+    ints_v[2:3, :] = jnp.maximum(up_to - 1, 0)
+    shifted = pltpu.roll(jnp.broadcast_to(sorted_target, (8, blocks)), 1, 1)[0:1]
+    joined = jnp.logical_and(shifted == sorted_target, ids > 0)
+    reals_v[0:1, :] = jnp.where(joined, 1.0, 0.0)
+    reals_v[1:2, :] = jnp.where(same > 0, 1.0, 0.0)
+    small = (pltpu.make_async_copy(ints_v, ints_s, small_sem.at[0]),
+             pltpu.make_async_copy(reals_v, reals_s, small_sem.at[1]))
+    for copy in small:
+        copy.start()
 
     lane = lax.broadcasted_iota(jnp.int32, (1, 128), 1)
 
@@ -51,7 +112,7 @@
         if field is not None:
             def one(r, carry):
                 peer = lax.rem(me + r, n)
-                outb[phase, peer] = field[want_s[peer]]
+                outb[phase, peer] = field[want_s[peer, 0, 0]]
                 pltpu.make_async_remote_copy(
                     src_ref=outb.at[phase, peer], dst_ref=inb.at[phase, me],
                     send_sem=send_sem.at[phase], recv_sem=recv_sem.at[phase],
@@ -60,7 +121,7 @@
                 return carry
 
             lax.fori_loop(1, n, one, 0)
-            inb[phase, me] = field[want_s[me]]
+            inb[phase, me] = field[want_s[me, 0, 0]]
         row = jnp.zeros((1, 128), f32)
         for i, (a, b) in enumerate(pairs):
             row = jnp.where(lane == i, jnp.broadcast_to(dot(a[...], b[...]), (1, 128)), row)
@@ -100,22 +161,20 @@
         def step(s, acc):
             for u in range(UNROLL // 2):
                 r = s * UNROLL + 2 * u
-                va, vb = vt[own_s[r]], vt[own_s[r + 1]]
+                va, vb = vt[ints_s[1, r]], vt[ints_s[1, r + 1]]
                 left = jnp.concatenate([jnp.concatenate([va, va], axis=1),
                                         jnp.concatenate([vb, vb], axis=1)], axis=0)
-                right = jnp.concatenate([w[perm_s[r]], w[perm_s[r + 1]]], axis=1)
+                right = jnp.concatenate([w[ints_s[0, r]], w[ints_s[0, r + 1]]], axis=1)
                 out = jnp.dot(left, right, preferred_element_type=f32)
-                acc = acc * keep_s[r] + (out[0:8, :cl] + out[8:16, :cl])
+                acc = acc * reals_s[0, r] + (out[0:8, :cl] + out[8:16, :cl])
                 runs[r] = acc
-                acc = acc * keep_s[r + 1] + (out[16:24, cl:] + out[24:32, cl:])
+                acc = acc * reals_s[0, r + 1] + (out[16:24, cl:] + out[24:32, cl:])
                 runs[r + 1] = acc
             return acc
 
         lax.fori_loop(0, blocks // UNROLL, step, jnp.zeros((8, cl), f32))
-        g = jnp.stack([runs[end_s[t]] * val_s[t] for t in range(clusters)])
+        g = jnp.stack([runs[ints_s[2, t]] * reals_s[1, t] for t in range(clusters)])
         return v - refl[...] * g
-
-    send(0, em, [(em, em)])
 
     def prepare(c, carry):
         slot = lax.rem(c, SLOTS)
@@ -125,7 +184,7 @@
             k = c * CHUNK + b
             t = stage[slot, b].T
             j = lax.broadcasted_iota(jnp.int32, (cl, cl), 0)
-            t = jnp.where(j < len_s[k], t, 0.0)
+            t = jnp.where(j < jnp.where(k < count_s[0], len_s[k], 0), t, 0.0)
             high = t.astype(bf16)
             w[k, 0:cl] = high
             w[k, cl:2 * cl] = (t - high.astype(f32)).astype(bf16)
@@ -139,7 +198,17 @@
 
         return carry
 
-    lax.fori_loop(0, chunks, prepare, 0)
+    early = min(EARLY, chunks)
+    lax.fori_loop(0, early, prepare, 0)
+    drain(win, wrecv_sem)
+    drain(wout, wsend_sem)
+    asked = pltpu.make_async_copy(win, want_s, small_sem.at[2])
+    asked.start()
+    asked.wait()
+    send(0, em, [(em, em)])
+    lax.fori_loop(early, chunks, prepare, 0)
+    for copy in small:
+        copy.wait()
 
     (rho,) = receive(0, 1, True)
     rs[...] = inb[0]
@@ -185,27 +254,6 @@
     blocks = form_factors.shape[0]
     devices = lax.axis_size(("gx", "gy"))
     i32, f32, bf16 = jnp.int32, jnp.float32, jnp.bfloat16
-    ids = jnp.arange(blocks, dtype=i32)
-    live = ids < block_count[0]
-    owner = link_source // clusters
-    slot = link_source % clusters
-    peers = jnp.arange(devices, dtype=i32)
-    match = (owner[None, :] == peers[:, None]) & live[None, :]
-    wanted = jnp.max(jnp.where(match, slot[None, :], 0), axis=1)
-    want = lax.all_to_all(wanted, ("gx", "gy"), split_axis=0, concat_axis=0, tiled=True)
-    length = jnp.where(live, link_length, 0)
-    target = link_target % clusters
-    key = target * blocks + ids
-    rank = jnp.sum((key[None, :] < key[:, None]).astype(i32), axis=1)
-    place = rank[None, :] == ids[:, None]
-    perm = jnp.sum(jnp.where(place, ids[None, :], 0), axis=1)
-    own = jnp.sum(jnp.where(place, owner[None, :], 0), axis=1)
-    sorted_target = jnp.sum(jnp.where(place, target[None, :], 0), axis=1)
-    before = jnp.concatenate([jnp.full((1,), -1, i32), sorted_target[:-1]])
-    keep = (before == sorted_target).astype(f32)
-    cids = jnp.arange(clusters, dtype=i32)
-    end = jnp.maximum(jnp.sum((target[None, :] <= cids[:, None]).astype(i32), axis=1) - 1, 0)
-    valid = jnp.any(target[None, :] == cids[:, None], axis=1).astype(f32)
     smem = pl.BlockSpec(memory_space=pltpu.SMEM)
     vmem = pl.BlockSpec(memory_space=pltpu.VMEM)
     field = (clusters, bands, cl)
@@ -214,7 +262,7 @@
     return pl.pallas_call(
         kernel,
         out_shape=[jax.ShapeDtypeStruct(field, f32)] * 2,
-        in_specs=[smem] * 7 + [vmem, vmem, pl.BlockSpec(memory_space=pl.ANY)],
+        in_specs=[smem] * 2 + [vmem] * 5 + [pl.BlockSpec(memory_space=pl.ANY)],
         out_specs=[vmem, vmem],
         scratch_shapes=[
             pltpu.VMEM((blocks, 2 * cl, cl), bf16),
@@ -231,16 +279,27 @@
             pltpu.VMEM(rows, f32),
             pltpu.VMEM(rows, f32),
             pltpu.VMEM(rows, f32),
+            pltpu.VMEM((devices, 1, 128), i32),
+            pltpu.VMEM((devices, 1, 128), i32),
+            pltpu.SMEM((devices, 1, 128), i32),
+            pltpu.VMEM((8, blocks), i32),
+            pltpu.SMEM((8, blocks), i32),
+            pltpu.VMEM((8, blocks), f32),
+            pltpu.SMEM((8, blocks), f32),
             dma((SLOTS,)),
             dma((PHASES,)),
             dma((PHASES,)),
             dma((PHASES,)),
             dma((PHASES,)),
+            dma,
+            dma,
+            dma((3,)),
         ],
         compiler_params=pltpu.CompilerParams(
             collective_id=0, has_side_effects=True, vmem_limit_bytes=56 * 1024 * 1024),
         name="radiosity",
-    )(perm, own, length, keep, end, valid, want, emission, reflectance, form_factors)
+    )(link_length, block_count, link_source.reshape(1, blocks), link_target.reshape(1, blocks),
+      block_count.reshape(1, 1), emission, reflectance, form_factors)
 
 
 def solution(mesh):

time: 101 us -> 80.4 us (0.80)
  starting transfers between devices: 7.33 us -> 0 us
  other arithmetic: 6.24 us -> 0 us
  Pallas kernels: 78.9 us -> 75.9 us
  waiting for transfers between devices: 2.84 us -> 0 us
    all_to_all x1 -> x0, starting transfers between devices: 7.33 us -> none  [local(): lax.all_to_all(wanted, ('gx', 'gy'), split_axis=0, concat_axis=0, tiled=T...]
    pallas_call x1, Pallas kernels: 78.9 us -> 75.9 us  [local(): pl.pallas_call(kernel, out_shape=[jax.ShapeDtypeStruct(field, f32)] * 2,...]
    all_to_all x1 -> x0, waiting for transfers between devices: 2.84 us -> none  [local(): lax.all_to_all(wanted, ('gx', 'gy'), split_axis=0, concat_axis=0, tiled=T...]
    select_n x2 -> x0, other arithmetic: 1.97 us -> none  [the longest x1 1.26 us: local(): length = jnp.where(live, link_length, 0)]
    convert_element_type x2 -> x0, other arithmetic: 1.22 us -> none  [the longest x1 0.64 us: local(): keep = (before == sorted_target).astype(f32)]
    all_to_all x1 -> x0, other arithmetic: 1.18 us -> none  [local(): lax.all_to_all(wanted, ('gx', 'gy'), split_axis=0, concat_axis=0, tiled=T...]
    reduce_sum x3 -> x0, other arithmetic: 1.09 us -> none  [the longest x1 0.8 us: local(): sorted_target = jnp.sum(jnp.where(place, target[None, :], 0), axis=1)]
  transfers between devices with their start and end apart: 1 -> 0, of which waited for: 1 -> 0; matrix products, arithmetic and copies ran while one was open for 4% -> 0% of each run, Pallas kernels for 0% -> 0%
where the time goes in v2:
time: 80.4 us; the launch traced here: 80.1 us
  Pallas kernels  75.9 us (94%)
  local copies, waits for them, and re-layouts  2.95 us (4%)
  between operations  1.29 us (2%)
    pallas_call x1, Pallas kernels, local(): pl.pallas_call(kernel, out_shape=[jax.ShapeDtypeStruct(field, f32)] * 2,...  75.9 us
    unnamed x2, local copies, waits for them, and re-layouts  2.95 us

profile of v2, /device:TPU:0, one launch (start us, length us, event | category | flops | bytes accessed | tf_op | source)
XLA Modules:
  0.0 80.1 jit_solution(12638800969060330936)
XLA Ops:
  1.3 75.9 %radiosity.1 = (f32[16,8,128]{2,1,0:T(8,128)}, f32[16,8,128]{2,1,0:T(8,128)}) custom-call(s32[256]{0:T(256)} %len_s.1, s32[1]{0:T(128)} %copy.11.count_s, s32[1,256]{1,0:T(1,128)} %bitcast.4, s32[1,256]{1,0:T(1,128)} %bitcast.5, s32[1,1]{1,0:T(1,128)} %bitcast.3.count_v, f32[16,8,128]{2,1,0:T(8,128)} %em.1, f32[16,8,128]{2,1,0:T(8,128)} %refl.1, ...), custom_call_target="tpu_custom_call" | custom-call | tf_op jit(solution)/shard_map/radiosity/pallas_call | solution.py:262
  77.2 1.5 %copy.12 = f32[16,8,128]{2,1,0:T(8,128)} copy(f32[16,8,128]{2,1,0:T(8,128)} %get-tuple-element.4) | data formatting | bytes 131072
  78.7 1.5 %copy.13 = f32[16,8,128]{2,1,0:T(8,128)} copy(f32[16,8,128]{2,1,0:T(8,128)} %get-tuple-element.5) | data formatting | bytes 131072

commit v3 on v2

--- a/solution.py
+++ b/solution.py
@@ -9,7 +9,7 @@
 PHASES = 2 * ITERS + 1
 CHUNK = 16
 SLOTS = 4
-UNROLL = 64
+UNROLL = 128
 EARLY = 4
 
 
@@ -22,7 +22,7 @@
 def kernel(len_s, count_s, source_v, target_v, count_v, em, refl, ff, sol, res,
            w, stage, runs, vt, outb, inb, dout, din, image, direction, total, rs, ds, ims,
            wout, win, want_s, ints_v, ints_s, reals_v, reals_s,
-           stage_sem, send_sem, recv_sem, dsend_sem, drecv_sem, wsend_sem, wrecv_sem, small_sem):
+           stage_sem, send_sem, recv_sem, wsend_sem, wrecv_sem, small_sem):
     nx, ny = lax.axis_size("gx"), lax.axis_size("gy")
     n = nx * ny
     me = lax.axis_index("gx") * ny + lax.axis_index("gy")
@@ -39,15 +39,23 @@
 
     barrier = pltpu.get_barrier_semaphore()
 
-    def greet(r, carry):
-        peer = lax.rem(me + r, n)
-        pl.semaphore_signal(barrier, inc=1, device_id=(peer // ny, lax.rem(peer, ny)),
-                            device_id_type=pl.DeviceIdType.MESH)
-        return carry
-
-    lax.fori_loop(1, n, greet, 0)
-
     i32 = jnp.int32
+    lane = lax.broadcasted_iota(i32, (1, 128), 1)
+    gx, gy = lax.axis_index("gx"), lax.axis_index("gy")
+
+    def each_peer(act):
+        def some(t, carry):
+            for a in range(nx):
+                act(lax.rem(gx + a, nx), lax.rem(gy + ny - 1 - t, ny))
+            return carry
+
+        lax.fori_loop(0, ny - 1, some, 0)
+        for a in range(1, nx):
+            act(lax.rem(gx + a, nx), gy)
+
+    each_peer(lambda px, py: pl.semaphore_signal(
+        barrier, inc=1, device_id=(px, py), device_id_type=pl.DeviceIdType.MESH))
+
     owner, slot = divide(source_v[...], clusters)
     target = target_v[...] - me * clusters
     ids = lax.broadcasted_iota(i32, (1, blocks), 1)
@@ -58,15 +66,9 @@
     wout[...] = jnp.broadcast_to(wanted, (n, 128)).reshape(n, 1, 128)
     pl.semaphore_wait(barrier, n - 1)
 
-    def ask(r, carry):
-        peer = lax.rem(me + r, n)
-        pltpu.make_async_remote_copy(
-            src_ref=wout.at[peer], dst_ref=win.at[me], send_sem=wsend_sem, recv_sem=wrecv_sem,
-            device_id=(peer // ny, lax.rem(peer, ny)),
-            device_id_type=pl.DeviceIdType.MESH).start()
-        return carry
-
-    lax.fori_loop(1, n, ask, 0)
+    each_peer(lambda px, py: pltpu.make_async_remote_copy(
+        src_ref=wout.at[px * ny + py], dst_ref=win.at[me], send_sem=wsend_sem, recv_sem=wrecv_sem,
+        device_id=(px, py), device_id_type=pl.DeviceIdType.MESH).start())
     win[me] = wout[me]
 
     square_of = (blocks, blocks)
@@ -101,57 +103,56 @@
     for copy in small:
         copy.start()
 
-    lane = lax.broadcasted_iota(jnp.int32, (1, 128), 1)
-
-    def dot(a, b):
-        part = jnp.sum(a * b, axis=0)
-        part = jnp.sum(part, axis=0, keepdims=True)
-        return jnp.sum(part, axis=1, keepdims=True)
-
-    def send(phase, field, pairs):
-        if field is not None:
-            def one(r, carry):
-                peer = lax.rem(me + r, n)
-                outb[phase, peer] = field[want_s[peer, 0, 0]]
-                pltpu.make_async_remote_copy(
-                    src_ref=outb.at[phase, peer], dst_ref=inb.at[phase, me],
-                    send_sem=send_sem.at[phase], recv_sem=recv_sem.at[phase],
-                    device_id=(peer // ny, lax.rem(peer, ny)),
-                    device_id_type=pl.DeviceIdType.MESH).start()
-                return carry
-
-            lax.fori_loop(1, n, one, 0)
-            inb[phase, me] = field[want_s[me, 0, 0]]
+    def fold(pairs):
         row = jnp.zeros((1, 128), f32)
         for i, (a, b) in enumerate(pairs):
-            row = jnp.where(lane == i, jnp.broadcast_to(dot(a[...], b[...]), (1, 128)), row)
-        dout[phase] = row
-        din[phase, me] = row
-
-        def two(r, carry):
-            peer = lax.rem(me + r, n)
+            part = jnp.sum(a[...] * b[...], axis=0)
+            part = part + pltpu.roll(part, 64, 1)
+            part = part + pltpu.roll(part, 32, 1)
+            part = jnp.sum(part, axis=0, keepdims=True)
+            row = jnp.where(lane // 32 == i, part, row)
+        return row
+
+    def send(phase, field, pairs):
+        row = fold(pairs)
+        if field is None:
+            dout[...] = row
+            din[me] = row
+        else:
+            inb[phase, me, 0:8] = field[want_s[me, 0, 0]]
+            inb[phase, me, 8:9] = row
+
+        def one(px, py):
+            peer = px * ny + py
+            if field is None:
+                src, dst = dout, din.at[me]
+            else:
+                outb[phase, peer, 0:8] = field[want_s[peer, 0, 0]]
+                outb[phase, peer, 8:9] = row
+                src, dst = outb.at[phase, peer], inb.at[phase, me]
             pltpu.make_async_remote_copy(
-                src_ref=dout.at[phase], dst_ref=din.at[phase, me],
-                send_sem=dsend_sem.at[phase], recv_sem=drecv_sem.at[phase],
-                device_id=(peer // ny, lax.rem(peer, ny)),
-                device_id_type=pl.DeviceIdType.MESH).start()
-            return carry
-
-        lax.fori_loop(1, n, two, 0)
+                src_ref=src, dst_ref=dst, send_sem=send_sem.at[phase], recv_sem=recv_sem.at[phase],
+                device_id=(px, py), device_id_type=pl.DeviceIdType.MESH).start()
+
+        each_peer(one)
 
     def drain(ref, sem):
         part = ref.at[pl.ds(0, n - 1)]
         pltpu.make_async_copy(part, part, sem).wait()
 
-    def receive(phase, count, rows):
-        drain(din.at[phase], drecv_sem.at[phase])
-        drain(din.at[phase], dsend_sem.at[phase])
-        sums = jnp.sum(din[phase], axis=0)
+    def receive(phase, rows):
         if rows:
             drain(inb.at[phase], recv_sem.at[phase])
             drain(outb.at[phase], send_sem.at[phase])
-        return [jnp.broadcast_to(jnp.sum(jnp.where(lane == i, sums, 0.0), axis=1, keepdims=True), (8, 128))
-                for i in range(count)]
+            return inb[phase, :, 8, :]
+        drain(din, recv_sem.at[phase])
+        drain(din, send_sem.at[phase])
+        return din[...].reshape(n, 128)
+
+    def whole(parts, i):
+        column = jnp.sum(parts, axis=0, keepdims=True)
+        return jnp.broadcast_to(
+            jnp.sum(jnp.where(lane // 32 == i, column, 0.0), axis=1, keepdims=True), (8, 128))
 
     def put_sources(v):
         low = v - v.astype(bf16).astype(f32)
@@ -210,8 +211,8 @@
     for copy in small:
         copy.wait()
 
-    (rho,) = receive(0, 1, True)
-    rs[...] = inb[0]
+    rho = whole(receive(0, True), 0)
+    rs[...] = inb[0, :, 0:8, :]
     res[...] = em[...]
     rho_old, alpha, omega = None, None, None
     for it in range(ITERS):
@@ -227,25 +228,24 @@
         image[...] = apply(direction[...])
         phase = 1 + 2 * it
         send(phase, image, [(em, image)])
-        (sim,) = receive(phase, 1, True)
-        alpha = rho / sim
-        ims[...] = inb[phase]
+        alpha = rho / whole(receive(phase, True), 0)
+        ims[...] = inb[phase, :, 0:8, :]
         res[...] = res[...] - alpha * image[...]
         rs[...] = rs[...] - alpha * ims[...]
         put_sources(rs[...])
         sol[...] = apply(res[...])
         send(phase + 1, None if last else sol, [(sol, res), (sol, sol), (em, res), (em, sol)])
-        cross, square, sm, sb = receive(phase + 1, 4, not last)
-        omega = cross / square
+        parts = receive(phase + 1, not last)
+        omega = whole(parts, 0) / whole(parts, 1)
         if it == 0:
             total[...] = alpha * direction[...] + omega * res[...]
         else:
             total[...] = total[...] + alpha * direction[...] + omega * res[...]
         res[...] = res[...] - omega * sol[...]
         if not last:
-            rs[...] = rs[...] - omega * inb[phase + 1]
+            rs[...] = rs[...] - omega * inb[phase + 1, :, 0:8, :]
         rho_old = rho
-        rho = sm - omega * sb
+        rho = whole(parts - omega[0:1] * pltpu.roll(parts, 96, 1), 2)
     sol[...] = total[...]
 
 
@@ -269,10 +269,10 @@
             pltpu.VMEM((SLOTS, CHUNK, cl, cl), f32),
             pltpu.VMEM((blocks, bands, cl), f32),
             pltpu.VMEM((devices, 2 * bands, cl), bf16),
-            pltpu.VMEM((PHASES - 1,) + rows, f32),
-            pltpu.VMEM((PHASES - 1,) + rows, f32),
-            pltpu.VMEM((PHASES, 1, 128), f32),
-            pltpu.VMEM((PHASES, devices, 1, 128), f32),
+            pltpu.VMEM((PHASES - 1, devices, bands + 1, cl), f32),
+            pltpu.VMEM((PHASES - 1, devices, bands + 1, cl), f32),
+            pltpu.VMEM((1, 128), f32),
+            pltpu.VMEM((devices, 1, 128), f32),
             pltpu.VMEM(field, f32),
             pltpu.VMEM(field, f32),
             pltpu.VMEM(field, f32),
@@ -289,8 +289,6 @@
             dma((SLOTS,)),
             dma((PHASES,)),
             dma((PHASES,)),
-            dma((PHASES,)),
-            dma((PHASES,)),
             dma,
             dma,
             dma((3,)),

time: 80.4 us -> 77.9 us (0.969)
  Pallas kernels: 75.9 us -> 73.4 us
    pallas_call x1, Pallas kernels: 75.9 us -> 73.4 us  [local(): pl.pallas_call(kernel, out_shape=[jax.ShapeDtypeStruct(field, f32)] * 2,...]
where the time goes in v3:
time: 77.9 us; the launch traced here: 77.6 us
  Pallas kernels  73.4 us (94%)
  local copies, waits for them, and re-layouts  2.95 us (4%)
  between operations  1.29 us (2%)
    pallas_call x1, Pallas kernels, local(): pl.pallas_call(kernel, out_shape=[jax.ShapeDtypeStruct(field, f32)] * 2,...  73.4 us
    unnamed x2, local copies, waits for them, and re-layouts  2.95 us

profile of v3, /device:TPU:0, one launch (start us, length us, event | category | flops | bytes accessed | tf_op | source)
XLA Modules:
  0.0 77.6 jit_solution(14429349432093076950)
XLA Ops:
  1.3 73.4 %radiosity.1 = (f32[16,8,128]{2,1,0:T(8,128)}, f32[16,8,128]{2,1,0:T(8,128)}) custom-call(s32[256]{0:T(256)} %len_s.1, s32[1]{0:T(128)} %copy.11.count_s, s32[1,256]{1,0:T(1,128)} %bitcast.4, s32[1,256]{1,0:T(1,128)} %bitcast.5, s32[1,1]{1,0:T(1,128)} %bitcast.3.count_v, f32[16,8,128]{2,1,0:T(8,128)} %em.1, f32[16,8,128]{2,1,0:T(8,128)} %refl.1, ...), custom_call_target="tpu_custom_call" | custom-call | tf_op jit(solution)/shard_map/radiosity/pallas_call | solution.py:262
  74.6 1.5 %copy.12 = f32[16,8,128]{2,1,0:T(8,128)} copy(f32[16,8,128]{2,1,0:T(8,128)} %get-tuple-element.4) | data formatting | bytes 131072
  76.1 1.5 %copy.13 = f32[16,8,128]{2,1,0:T(8,128)} copy(f32[16,8,128]{2,1,0:T(8,128)} %get-tuple-element.5) | data formatting | bytes 131072
